TPU v7x, 32 devices: a whole 2x2x4 slice. The times are simulated.
32 devices in a mesh: seq: 8 (over z, x), tp: 4 (over y, core).
Axes of the slice: x: 2, y: 2, z: 4, core: 2. Of those that a mesh axis runs over, the one named last changes fastest.
Arguments:
- queries: bfloat16 [1536, 6144], P('seq', 'tp'), may hold values from -400 to 400
- key_vectors: bfloat16 [1536, 1024], P('seq', 'tp'), may hold values from -8 to 8
- value_vectors: bfloat16 [1536, 1024], P('seq', 'tp'), may hold values from -6 to 6
- positions: int32 [1536], P('seq'), may hold values from 0 to 1535, as said below
- residual: bfloat16 [1536, 6144], P('seq', 'tp'), may hold values from -200 to 200
- norm_gain: float32 [1, 6144], P(None, 'tp'), may hold values from 0.5 to 1.5
- out_weight: bfloat16 [6144, 6144], P('tp'), may hold values from -0.3125 to 0.3125
Outputs:
- quantized: bfloat16 [1536, 6144], P('seq')
- token_scale: float32 [1536], P('seq')
- new_residual: bfloat16 [1536, 6144], P('seq', 'tp')
Inputs may be any that keep to these rules, and one draw needn't show every extreme that they name: The positions are a permutation of 0 to 1535. Cut into 16 runs of 96 consecutive positions, the rows of one index of seq hold run r in their first 96 rows and run 2 * 8 - 1 - r in their last ones, both in increasing order, with r differing between the indices of seq.
All inputs are finite; a program needn't handle non-finite values. Where the computation divides by a largest or mean magnitude, that divisor is 1e-20 or more.
Results may differ from a plain program's by a relative error of at most 0.012.
Values may be sent and summed in bfloat16 or wider, within the bound.
A program may use at most 64 MiB of HBM per device.

v0:
```python
import math
import jax
import jax.numpy as jnp
from jax import lax
from jax.sharding import PartitionSpec as P

D = 6144
Q_HEADS = 48
KV_HEADS = 8
HEAD = 128
NEG_FILL = -1e30


def fresh_state(kv_count, state_rows):
    return (
        jnp.full((kv_count, state_rows), NEG_FILL, jnp.float32),
        jnp.zeros((kv_count, state_rows), jnp.float32),
        jnp.zeros((kv_count, state_rows, HEAD), jnp.float32),
    )


def attend(state_now, query_part, half_rows_pos, key_block, value_block, key_pos):
    running_max, running_sum, weighted_sum = state_now
    kv_count = query_part.shape[0]
    group_size = Q_HEADS // KV_HEADS
    score_scale = 1.0 / math.sqrt(HEAD)
    query_pos = jnp.tile(half_rows_pos, group_size)
    key_heads = key_block.reshape(key_block.shape[0], kv_count, HEAD)
    value_heads = value_block.reshape(value_block.shape[0], kv_count, HEAD)
    scores = (
        jnp.einsum("kmd,skd->kms", query_part, key_heads, preferred_element_type=jnp.float32)
        * score_scale
    )
    visible = key_pos[None, :] <= query_pos[:, None]
    scores = jnp.where(visible[None], scores, NEG_FILL)
    new_max = jnp.maximum(running_max, jnp.max(scores, axis=2))
    weights = jnp.where(visible[None], jnp.exp(scores - new_max[..., None]), 0.0)
    factor = jnp.exp(running_max - new_max)
    running_sum = running_sum * factor + jnp.sum(weights, axis=2)
    weighted_sum = weighted_sum * factor[..., None] + jnp.einsum(
        "kms,skd->kmd",
        weights.astype(jnp.bfloat16),
        value_heads,
        preferred_element_type=jnp.float32,
    )
    return (new_max, running_sum, weighted_sum)


def fold_block(states, halves, half_pos, key_block, value_block, key_pos):
    result = []
    for half_index in range(2):

        def compute(state_now, half_index=half_index):
            return attend(
                state_now, halves[half_index], half_pos[half_index], key_block, value_block, key_pos
            )

        result.append(compute(states[half_index]))
    return tuple(result)


def fold_piece(states, halves, half_pos, key_piece, value_piece, key_pos):
    row_count = key_piece.shape[0]
    block_rows = math.gcd(row_count, 1024)
    block_count = row_count // block_rows

    def scan_step(loop_carry, block_pair):
        return (
            fold_block(loop_carry, halves, half_pos, block_pair[0], block_pair[1], block_pair[2]),
            None,
        )

    stacked = (
        key_piece.reshape(block_count, block_rows, key_piece.shape[1]),
        value_piece.reshape(block_count, block_rows, value_piece.shape[1]),
        key_pos.reshape(block_count, block_rows),
    )
    states, unused = lax.scan(scan_step, states, stacked)
    return states


def on_device(queries, key_vectors, value_vectors, positions, residual, norm_gain, out_weight):
    token_rows = queries.shape[0]
    run_rows = token_rows // 2
    group_size = Q_HEADS // KV_HEADS
    kv_count = key_vectors.shape[1] // HEAD
    query_split = queries.reshape(2, run_rows, kv_count, group_size, HEAD).transpose(0, 2, 3, 1, 4)
    query_split = query_split.reshape(2, kv_count, group_size * run_rows, HEAD)
    halves = (query_split[0], query_split[1])
    half_pos = (positions[:run_rows], positions[run_rows:])
    initial = (
        fresh_state(kv_count, group_size * run_rows),
        fresh_state(kv_count, group_size * run_rows),
    )
    all_pos = lax.all_gather(positions, "seq", axis=0, tiled=True)
    kv_pair = jnp.stack((key_vectors, value_vectors))
    pieces = lax.all_gather(kv_pair, "seq", axis=1, tiled=True)
    states = fold_piece(initial, halves, half_pos, pieces[0], pieces[1], all_pos)
    outputs = []
    for state_now in states:
        outputs.append((state_now[2] / state_now[1][..., None]).astype(jnp.bfloat16))
    attended = (
        jnp.stack(outputs).reshape(2, kv_count, group_size, run_rows, HEAD).transpose(0, 3, 1, 2, 4)
    )
    attended = attended.reshape(token_rows, kv_count * group_size * HEAD)
    partial_value = jnp.dot(attended, out_weight, preferred_element_type=jnp.float32)
    partial_value = partial_value.astype(jnp.bfloat16).astype(jnp.float32)
    summed = lax.psum_scatter(
        partial_value.astype(jnp.bfloat16), "tp", scatter_dimension=1, tiled=True
    ).astype(jnp.float32) + residual.astype(jnp.float32)
    square_sum = lax.psum(jnp.sum(summed * summed, axis=1), "tp")
    normed = summed * lax.rsqrt(square_sum / D + 1e-05)[:, None] * norm_gain
    peak_value = lax.pmax(jnp.max(jnp.abs(normed), axis=1), "tp") + 1e-06
    local_scaled = (normed / peak_value[:, None]).astype(jnp.bfloat16)
    quantized = lax.all_gather(local_scaled, "tp", axis=1, tiled=True)
    new_residual = summed.astype(jnp.bfloat16)
    return (quantized, peak_value, new_residual)


def solution(mesh):
    return jax.shard_map(
        on_device,
        mesh=mesh,
        in_specs=(
            P("seq", "tp"),
            P("seq", "tp"),
            P("seq", "tp"),
            P("seq"),
            P("seq", "tp"),
            P(None, "tp"),
            P("tp", None),
        ),
        out_specs=(P("seq", None), P("seq"), P("seq", "tp")),
        check_vma=False,
    )
```

profile of v0, /device:TPU:0, one launch (start us, length us, event | category | flops | bytes accessed | tf_op | source)
XLA Modules:
  0.0 205.4 jit_solution(1911410734703839984)
XLA Ops:
  7.2 1.6 pad_maximum_fusion
  9.0 1.8 reshape.108
  11.0 0.8 copy.22
  13.3 13.5 %all-reduce = s32[1536]{0:T(1024)S(1)} all-reduce(s32[1536]{0:T(1024)S(1)} %dynamic-update-slice), channel_id=1, replica_groups=mesh['seq'=8,'tp'=4] {'seq'}, use_global_device_ids=true, to_apply=%add | all-reduce | flops 1536 | bytes 12288
  28.1 29.7 %all-gather.3.cloned.1.call-done = bf16[2,1536,256]{2,1,0:T(8,128)(2,1)} async-done(((bf16[2,192,256]{2,1,0:T(8,128)(2,1)}), bf16[2,1536,256]{2,1,0:T(8,128)(2,1)}) %all-gather.3.cloned.1.call-update) | async-done | bytes 1572880 | tf_op jit(solution)/shard_map/all_gather | solution.py:97
  57.7 2.6 %fusion.27 = (bf16[1,1536,256]{2,1,0:T(8,128)(2,1)}, bf16[1,1536,256]{2,1,0:T(8,128)(2,1)}) fusion(bf16[2,1536,256]{2,1,0:T(8,128)(2,1)} %all-gather.3.cloned.1.call-done), kind=kLoop, calls=%fused_computation.56 | loop fusion | bytes 3145728 | tf_op jit(solution)/shard_map/slice | solution.py:98
  60.4 48.9 %while.21 = (s32[]{:T(128)}, f32[2,576]{1,0:T(2,128)S(1)}, f32[2,576]{1,0:T(2,128)S(1)}, f32[2,576,128]{2,1,0:T(8,128)}, f32[2,576]{1,0:T(2,128)S(1)}, /*index=5...) while((s32[]{:T(128)}, f32[2,576]{1,0:T(2,128)S(1)}, ...), condition=%wide.region_5.6_spmd.clone, body=%wide.region_0.5_spmd.clone.sunk | while | flops 620801280 | bytes 39185492 | solution.py:78
  60.4 0.7 constant_dynamic-slice_fusion.6
  62.9 1.0 constant_dynamic-slice_fusion.7
  64.8 1.0 fusion.66
  66.5 1.4 copy-done
  67.8 1.0 fusion.65
  69.4 1.0 constant_dynamic-slice_fusion.8
  70.4 0.8 copy.36
  71.2 3.5 %convolution_add_fusion.5 = f32[2,576,128]{2,1,0:T(8,128)} fusion(bf16[512,2,128]{0,2,1:T(8,128)(2,1)} %bitcast.79, f32[2,512,576]{1,2,0:T(8,128)} %copy-done, f32[2,576]{1,0:T(2,128)S(1)} %fusion.64, pred[576,512]{1,0:T(8,128)(4,1)S(1)} %get-tuple-element.288, f32[2,576,128]{2,1,0:T(8,128)} %get-tuple-element.318, ...), kind=kOutput, calls=%fused_computation.10.clone.1 | convolution fusion | flops 154386432 | bytes 4105217 | tf_op jit(solution)/shard_map/while/body/eval_jaxpr/kms,skd->kmd/dot_general | solution.py:40
  74.7 1.0 convolution_add_fusion.4
  75.7 0.8 copy-done.6
  76.5 0.7 constant_dynamic-slice_fusion.6
  79.1 1.0 constant_dynamic-slice_fusion.7
  80.9 1.0 fusion.66
  81.9 0.7 fusion.63
  82.6 1.4 copy-done
  84.0 1.0 fusion.65
  85.6 1.0 constant_dynamic-slice_fusion.8
  86.6 0.8 copy.36
  87.4 3.7 %convolution_add_fusion.5 = f32[2,576,128]{2,1,0:T(8,128)} fusion(bf16[512,2,128]{0,2,1:T(8,128)(2,1)} %bitcast.79, f32[2,512,576]{1,2,0:T(8,128)} %copy-done, f32[2,576]{1,0:T(2,128)S(1)} %fusion.64, pred[576,512]{1,0:T(8,128)(4,1)S(1)} %get-tuple-element.288, f32[2,576,128]{2,1,0:T(8,128)} %get-tuple-element.318, ...), kind=kOutput, calls=%fused_computation.10.clone.1 | convolution fusion | flops 154386432 | bytes 4105217 | tf_op jit(solution)/shard_map/while/body/eval_jaxpr/kms,skd->kmd/dot_general | solution.py:40
  91.1 1.0 convolution_add_fusion.4
  92.1 0.8 copy-done.6
  92.9 0.7 constant_dynamic-slice_fusion.6
  95.5 1.0 constant_dynamic-slice_fusion.7
  97.3 1.0 fusion.66
  99.0 1.4 copy-done
  100.4 1.0 fusion.65
  102.0 1.0 constant_dynamic-slice_fusion.8
  102.9 0.8 copy.36
  103.8 3.7 %convolution_add_fusion.5 = f32[2,576,128]{2,1,0:T(8,128)} fusion(bf16[512,2,128]{0,2,1:T(8,128)(2,1)} %bitcast.79, f32[2,512,576]{1,2,0:T(8,128)} %copy-done, f32[2,576]{1,0:T(2,128)S(1)} %fusion.64, pred[576,512]{1,0:T(8,128)(4,1)S(1)} %get-tuple-element.288, f32[2,576,128]{2,1,0:T(8,128)} %get-tuple-element.318, ...), kind=kOutput, calls=%fused_computation.10.clone.1 | convolution fusion | flops 154386432 | bytes 4105217 | tf_op jit(solution)/shard_map/while/body/eval_jaxpr/kms,skd->kmd/dot_general | solution.py:40
  107.4 1.0 convolution_add_fusion.4
  108.4 0.8 copy-done.6
  109.2 1.6 divide_convert_fusion.1
  112.0 11.6 %convolution_convert_fusion = bf16[192,6144]{1,0:T(8,128)(2,1)} fusion(bf16[192,1536]{1,0:T(8,128)(2,1)S(1)} %reshape.109, bf16[1536,6144]{1,0:T(8,128)(2,1)} %param.15), kind=kOutput, calls=%fused_computation.43 | convolution fusion | flops 3625058304 | bytes 21823488 | tf_op jit(solution)/shard_map/dot_general | solution.py:106
  124.3 30.6 %reduce-scatter.2.cloned.1.call-done = bf16[192,1536]{1,0:T(8,128)(2,1)} async-done(((bf16[192,6144]{1,0:T(8,128)(2,1)}), bf16[192,1536]{1,0:T(8,128)(2,1)}) %reduce-scatter.2.cloned.1.call-update) | async-done | bytes 589840 | tf_op jit(solution)/shard_map/reduce_scatter | solution.py:108
  154.9 1.4 multiply_reduce_fusion
  156.3 5.8 %psum.7 = f32[192]{0:T(256)S(1)} all-reduce(f32[192]{0:T(256)S(1)} %multiply_reduce_fusion), channel_id=1, replica_groups=mesh['seq'=8,'tp'=4] {'tp'}, use_global_device_ids=true, to_apply=%region_8.9 | all-reduce | flops 192 | bytes 1536 | tf_op jit(solution)/shard_map/psum | solution.py:111
  162.1 1.4 abs_reduce_fusion
  163.5 5.7 %pmax.7 = f32[192]{0:T(256)S(1)} all-reduce(f32[192]{0:T(256)S(1)} %abs_reduce_fusion), channel_id=1, replica_groups=mesh['seq'=8,'tp'=4] {'tp'}, use_global_device_ids=true, to_apply=%region_10.11 | all-reduce | flops 192 | bytes 1536 | tf_op jit(solution)/shard_map/pmax | solution.py:113
  169.2 1.3 fusion.26
  170.5 25.0 %all-gather.5.cloned.1.call-done = bf16[192,6144]{1,0:T(8,128)(2,1)} async-done(((bf16[192,1536]{1,0:T(8,128)(2,1)}), bf16[192,6144]{1,0:T(8,128)(2,1)}) %all-gather.5.cloned.1.call-update) | async-done | bytes 2359312 | tf_op jit(solution)/shard_map/all_gather | solution.py:115
  195.5 3.3 %copy.60 = bf16[192,6144]{1,0:T(8,128)(2,1)} copy(bf16[192,6144]{1,0:T(8,128)(2,1)} %all-gather.5.cloned.1.call-done) | data formatting | bytes 4718592
  (106 shorter events, 15.7 us)
Async XLA Ops:
  7.2 50.6 %all-gather.3.cloned.1.call-start = ((), (), s32[]{:S(2)}) async-start(), calls=%async_computation.1 | async-start | bytes 1769472 | tf_op jit(solution)/shard_map/all_gather | solution.py:97
  8.8 2.9 %copy-start.11 = (u32[32]{0:T(128)S(1)}, u32[32]{0:T(128)}, u32[]{:S(2)}) copy-start(u32[32]{0:T(128)} %constant.37) | copy-start | bytes 388
  8.9 4.2 %copy-start.10 = (s32[192]{0:T(256)S(1)}, s32[192]{0:T(256)}, u32[]{:S(2)}) copy-start(s32[192]{0:T(256)} %param.12) | copy-start | bytes 2308
  8.9 146.0 %reduce-scatter.2.cloned.1.call-start = ((), (), s32[]{:S(2)}) async-start(), calls=%async_computation.2 | async-start | bytes 2949120 | tf_op jit(solution)/shard_map/reduce_scatter | solution.py:108
  64.8 1.0 copy-start.1
  66.4 1.4 copy-start
  71.2 3.5 %copy-start.2 = (bf16[1,512,256]{1,2,0:T(8,128)(2,1)S(1)}, bf16[1,512,256]{1,2,0:T(8,128)(2,1)}, u32[]{:S(2)}) copy-start(bf16[1,512,256]{1,2,0:T(8,128)(2,1)} %copy.36) | copy-start | bytes 786436 | tf_op jit(solution)/shard_map/while
  71.2 3.5 %copy-start.5 = (f32[2,576,128]{2,1,0:T(8,128)S(1)}, f32[2,576,128]{2,1,0:T(8,128)}, u32[]{:S(2)}) copy-start(f32[2,576,128]{2,1,0:T(8,128)} %get-tuple-element.315) | copy-start | bytes 1769476 | tf_op jit(solution)/shard_map/while
  71.2 3.5 %copy-start.7 = (f32[2,576]{1,0:T(2,128)S(1)}, f32[2,576]{1,0:T(2,128)}, u32[]{:S(2)}) copy-start(f32[2,576]{1,0:T(2,128)} %get-tuple-element.293) | copy-start | bytes 13828 | tf_op jit(solution)/shard_map/while
  75.7 0.8 copy-start.6
  80.9 1.0 copy-start.1
  82.6 1.4 copy-start
  87.4 3.7 %copy-start.2 = (bf16[1,512,256]{1,2,0:T(8,128)(2,1)S(1)}, bf16[1,512,256]{1,2,0:T(8,128)(2,1)}, u32[]{:S(2)}) copy-start(bf16[1,512,256]{1,2,0:T(8,128)(2,1)} %copy.36) | copy-start | bytes 786436 | tf_op jit(solution)/shard_map/while
  87.4 3.7 %copy-start.5 = (f32[2,576,128]{2,1,0:T(8,128)S(1)}, f32[2,576,128]{2,1,0:T(8,128)}, u32[]{:S(2)}) copy-start(f32[2,576,128]{2,1,0:T(8,128)} %get-tuple-element.315) | copy-start | bytes 1769476 | tf_op jit(solution)/shard_map/while
  87.4 3.7 %copy-start.7 = (f32[2,576]{1,0:T(2,128)S(1)}, f32[2,576]{1,0:T(2,128)}, u32[]{:S(2)}) copy-start(f32[2,576]{1,0:T(2,128)} %get-tuple-element.293) | copy-start | bytes 13828 | tf_op jit(solution)/shard_map/while
  92.1 0.8 copy-start.6
  97.3 1.0 copy-start.1
  98.9 1.4 copy-start
  103.8 3.7 %copy-start.2 = (bf16[1,512,256]{1,2,0:T(8,128)(2,1)S(1)}, bf16[1,512,256]{1,2,0:T(8,128)(2,1)}, u32[]{:S(2)}) copy-start(bf16[1,512,256]{1,2,0:T(8,128)(2,1)} %copy.36) | copy-start | bytes 786436 | tf_op jit(solution)/shard_map/while
  103.8 3.7 %copy-start.5 = (f32[2,576,128]{2,1,0:T(8,128)S(1)}, f32[2,576,128]{2,1,0:T(8,128)}, u32[]{:S(2)}) copy-start(f32[2,576,128]{2,1,0:T(8,128)} %get-tuple-element.315) | copy-start | bytes 1769476 | tf_op jit(solution)/shard_map/while
  103.8 3.7 %copy-start.7 = (f32[2,576]{1,0:T(2,128)S(1)}, f32[2,576]{1,0:T(2,128)}, u32[]{:S(2)}) copy-start(f32[2,576]{1,0:T(2,128)} %get-tuple-element.293) | copy-start | bytes 13828 | tf_op jit(solution)/shard_map/while
  108.4 0.8 copy-start.6
  123.6 0.7 copy-start.8
  123.6 31.3 %copy-start.3 = (bf16[192,1536]{1,0:T(8,128)(2,1)S(1)}, bf16[192,1536]{1,0:T(8,128)(2,1)}, u32[]{:S(2)}) copy-start(bf16[192,1536]{1,0:T(8,128)(2,1)} %param.13) | copy-start | bytes 1769476
  123.6 71.9 %all-gather.5.cloned.1.call-start = ((), (), s32[]{:S(2)}) async-start(), calls=%async_computation.3 | async-start | bytes 2949120 | tf_op jit(solution)/shard_map/all_gather | solution.py:115
  154.9 14.3 %copy-start.4 = (bf16[192,1536]{1,0:T(8,128)(2,1)S(1)}, bf16[192,1536]{1,0:T(8,128)(2,1)}, u32[]{:S(2)}) copy-start(bf16[192,1536]{1,0:T(8,128)(2,1)} %reduce-scatter.2.cloned.1.call-done) | copy-start | bytes 1769476
  169.2 29.7 %copy-start.9 = (f32[192]{0:T(256)}, f32[192]{0:T(256)S(1)}, u32[]{:S(2)}) copy-start(f32[192]{0:T(256)S(1)} %broadcast_add_fusion) | copy-start | bytes 2308
Sparse Core Ops, SparseCore 0:
  10.7 46.9 all-gather.2
  123.7 31.1 reduce-scatter.1
  170.6 24.8 all-gather.4
where the time goes:
time: 206 us; the launch traced here: 205 us
  waiting for transfers between devices  85.3 us (41%)
  local copies, waits for them, and re-layouts  34.3 us (17%)
  matrix products  29.4 us (14%)
  blocking collectives  24.9 us (12%)
  other arithmetic  16.5 us (8%)
  between operations  14.5 us (7%)
    reduce_scatter x1, waiting for transfers between devices, on_device(): lax.psum_scatter(partial_value.astype(jnp.bfloat16), 'tp', scatter_dimens...  30.6 us
    all_gather x1, waiting for transfers between devices, on_device(): pieces = lax.all_gather(kv_pair, 'seq', axis=1, tiled=True)  29.7 us
    all_gather x1, waiting for transfers between devices, on_device(): quantized = lax.all_gather(local_scaled, 'tp', axis=1, tiled=True)  25 us
    dot_general x6, matrix products, attend(): jnp.einsum('kms,skd->kmd', weights.astype(jnp.bfloat16), value_heads, pre...  13.7 us
    unnamed x1, blocking collectives  13.5 us
    dot_general x1, matrix products, on_device(): jnp.dot(attended, out_weight, preferred_element_type=jnp.float32)  11.6 us
    dynamic_slice x15, local copies, waits for them, and re-layouts, fold_piece(): states, unused = lax.scan(scan_step, states, stacked)  10.9 us
    while x42, local copies, waits for them, and re-layouts  6.63 us
  transfers between devices with their start and end apart: 3, of which 3 were waited for; matrix products, arithmetic and copies ran while one was open for 2% of the time, Pallas kernels for 0%

commit v1 on v0

--- a/solution.py
+++ b/solution.py
@@ -112,7 +112,12 @@
     normed = summed * lax.rsqrt(square_sum / D + 1e-05)[:, None] * norm_gain
     peak_value = lax.pmax(jnp.max(jnp.abs(normed), axis=1), "tp") + 1e-06
     local_scaled = (normed / peak_value[:, None]).astype(jnp.bfloat16)
-    quantized = lax.all_gather(local_scaled, "tp", axis=1, tiled=True)
+    ring = [local_scaled]
+    for hop in range(3):
+        ring.append(lax.ppermute(ring[-1], "tp", [(dev, (dev + 1) % 4) for dev in range(4)]))
+    quantized = jnp.roll(
+        jnp.concatenate(ring[::-1], axis=1), (lax.axis_index("tp") + 1) * ring[0].shape[1], axis=1
+    )
     new_residual = summed.astype(jnp.bfloat16)
     return (quantized, peak_value, new_residual)
 

time: 206 us -> 193 us (0.937)
  matrix products: 29.4 us -> 21.5 us
  local copies, waits for them, and re-layouts: 34.3 us -> 26.5 us
  waiting for transfers between devices: 85.3 us -> 87.7 us
    ppermute x0 -> x3, waiting for transfers between devices: none -> 27.9 us  [on_device(): lax.ppermute(ring[-1], 'tp', [(dev, (dev + 1) % 4) for dev in range(4)])]
    all_gather x1 -> x0, waiting for transfers between devices: 25 us -> none  [on_device(): quantized = lax.all_gather(local_scaled, 'tp', axis=1, tiled=True)]
    dot_general x6, matrix products: 13.7 us -> 5.82 us  [attend(): jnp.einsum('kms,skd->kmd', weights.astype(jnp.bfloat16), value_heads, pre...]
    dynamic_slice x15, local copies, waits for them, and re-layouts: 10.9 us -> 4.84 us  [fold_piece(): states, unused = lax.scan(scan_step, states, stacked)]
    while x42, local copies, waits for them, and re-layouts: 6.63 us -> 2.63 us
    le x6, local copies, waits for them, and re-layouts: 0.45 us -> 4.01 us  [attend(): visible = key_pos[None, :] <= query_pos[:, None]]
    dynamic_slice x0 -> x1, local copies, waits for them, and re-layouts: none -> 2.27 us  [on_device(): jnp.roll(jnp.concatenate(ring[::-1], axis=1), (lax.axis_index('tp') + 1)...]
    le x3, other arithmetic: 1.2 us -> 3.3 us  [attend(): visible = key_pos[None, :] <= query_pos[:, None]]
  transfers between devices with their start and end apart: 3 -> 5, of which waited for: 3 -> 5; matrix products, arithmetic and copies ran while one was open for 2% -> 3% of each run, Pallas kernels for 0% -> 0%
where the time goes in v1:
time: 193 us; the launch traced here: 192 us
  waiting for transfers between devices  87.7 us (45%)
  local copies, waits for them, and re-layouts  26.5 us (14%)
  blocking collectives  24.8 us (13%)
  matrix products  21.5 us (11%)
  other arithmetic  16.5 us (9%)
  between operations  14.9 us (8%)
    reduce_scatter x1, waiting for transfers between devices, on_device(): lax.psum_scatter(partial_value.astype(jnp.bfloat16), 'tp', scatter_dimens...  30.6 us
    all_gather x1, waiting for transfers between devices, on_device(): pieces = lax.all_gather(kv_pair, 'seq', axis=1, tiled=True)  29.2 us
    ppermute x3, waiting for transfers between devices, on_device(): lax.ppermute(ring[-1], 'tp', [(dev, (dev + 1) % 4) for dev in range(4)])  27.9 us
    unnamed x1, blocking collectives  13.3 us
    dot_general x1, matrix products, on_device(): jnp.dot(attended, out_weight, preferred_element_type=jnp.float32)  11.6 us
    reduce_sum x6, other arithmetic, attend(): running_sum = running_sum * factor + jnp.sum(weights, axis=2)  5.85 us
    dot_general x6, matrix products, attend(): jnp.einsum('kms,skd->kmd', weights.astype(jnp.bfloat16), value_heads, pre...  5.82 us
    psum x1, blocking collectives, on_device(): square_sum = lax.psum(jnp.sum(summed * summed, axis=1), 'tp')  5.75 us
  transfers between devices with their start and end apart: 5, of which 5 were waited for; matrix products, arithmetic and copies ran while one was open for 3% of the time, Pallas kernels for 0%

profile of v1, /device:TPU:0, one launch (start us, length us, event | category | flops | bytes accessed | tf_op | source)
XLA Modules:
  0.0 192.4 jit_solution(11197326863092627866)
XLA Ops:
  7.2 1.6 pad_maximum_fusion
  9.0 1.3 dynamic-slice
  10.9 0.9 dynamic-update-slice
  11.8 13.3 %all-reduce = s32[1536]{0:T(1024)S(1)} all-reduce(s32[1536]{0:T(1024)S(1)} %dynamic-update-slice), channel_id=1, replica_groups=mesh['seq'=8,'tp'=4] {'seq'}, use_global_device_ids=true, to_apply=%add | all-reduce | flops 1536 | bytes 12288
  25.7 1.8 reshape.108
  28.5 29.2 %all-gather.2.cloned.1.call-done = bf16[2,1536,256]{2,1,0:T(8,128)(2,1)} async-done(((bf16[2,192,256]{2,1,0:T(8,128)(2,1)}), bf16[2,1536,256]{2,1,0:T(8,128)(2,1)}) %all-gather.2.cloned.1.call-update) | async-done | bytes 1572880 | tf_op jit(solution)/shard_map/all_gather | solution.py:97
  57.7 1.5 fusion.27
  59.1 34.9 %while.21 = (s32[]{:T(128)}, f32[2,576]{1,0:T(2,128)S(1)}, f32[2,576]{1,0:T(2,128)}, f32[2,576,128]{2,1,0:T(8,128)}, f32[2,576]{1,0:T(2,128)S(1)}, /*index=5*/f3...) while((s32[]{:T(128)}, f32[2,576]{1,0:T(2,128)S(1)}, ...), condition=%wide.region_5.6_spmd.clone, body=%wide.region_0.5_spmd.clone.sunk | while | flops 620801280 | bytes 27575388 | solution.py:78
  59.2 1.3 constant_dynamic-slice_fusion.7
  63.4 1.1 broadcast_compare_fusion.3
  64.5 0.7 fusion.61
  65.2 1.0 fusion.66
  66.2 0.7 fusion.63
  66.9 1.0 fusion.65
  67.9 1.0 convolution_add_fusion.5
  69.0 1.0 convolution_add_fusion.4
  70.0 0.8 copy-done.3
  70.8 1.3 constant_dynamic-slice_fusion.7
  74.0 0.7 le.58
  75.0 1.1 broadcast_compare_fusion.3
  76.1 0.7 fusion.61
  76.8 1.0 fusion.66
  77.8 0.7 fusion.63
  78.5 1.0 fusion.65
  79.5 1.0 convolution_add_fusion.5
  80.6 1.0 convolution_add_fusion.4
  81.6 0.8 copy-done.3
  82.4 1.3 constant_dynamic-slice_fusion.7
  86.6 1.1 broadcast_compare_fusion.3
  87.7 0.7 fusion.61
  88.4 1.0 fusion.66
  89.4 0.7 fusion.63
  90.1 1.0 fusion.65
  91.1 1.0 convolution_add_fusion.5
  92.2 1.0 convolution_add_fusion.4
  93.2 0.8 copy-done.3
  94.0 1.4 divide_convert_fusion.1
  96.6 11.6 %convolution_convert_fusion = bf16[192,6144]{1,0:T(8,128)(2,1)} fusion(bf16[192,1536]{1,0:T(8,128)(2,1)S(1)} %reshape.109, bf16[1536,6144]{1,0:T(8,128)(2,1)} %param.15), kind=kOutput, calls=%fused_computation.43 | convolution fusion | flops 3625058304 | bytes 21823488 | tf_op jit(solution)/shard_map/dot_general | solution.py:106
  108.9 30.6 %reduce-scatter.2.cloned.1.call-done = bf16[192,1536]{1,0:T(8,128)(2,1)} async-done(((bf16[192,6144]{1,0:T(8,128)(2,1)}), bf16[192,1536]{1,0:T(8,128)(2,1)}) %reduce-scatter.2.cloned.1.call-update) | async-done | bytes 589840 | tf_op jit(solution)/shard_map/reduce_scatter | solution.py:108
  139.5 1.4 multiply_reduce_fusion
  140.9 5.8 %psum.7 = f32[192]{0:T(256)S(1)} all-reduce(f32[192]{0:T(256)S(1)} %multiply_reduce_fusion), channel_id=1, replica_groups=mesh['seq'=8,'tp'=4] {'tp'}, use_global_device_ids=true, to_apply=%region_8.9 | all-reduce | flops 192 | bytes 1536 | tf_op jit(solution)/shard_map/psum | solution.py:111
  146.7 1.4 abs_reduce_fusion
  148.1 5.7 %pmax.7 = f32[192]{0:T(256)S(1)} all-reduce(f32[192]{0:T(256)S(1)} %abs_reduce_fusion), channel_id=1, replica_groups=mesh['seq'=8,'tp'=4] {'tp'}, use_global_device_ids=true, to_apply=%region_10.11 | all-reduce | flops 192 | bytes 1536 | tf_op jit(solution)/shard_map/pmax | solution.py:113
  153.8 1.1 fusion.26
  154.9 9.3 %collective-permute-done = bf16[192,1536]{1,0:T(8,128)(2,1)S(1)} collective-permute-done((bf16[192,1536]{1,0:T(8,128)(2,1)S(1)}, bf16[192,1536]{1,0:T(8,128)(2,1)S(1)}, u32[]{:S(2)}, u32[]{:S(2)}) %collective-permute-start) | collective-permute-done | bytes 589856 | tf_op jit(solution)/shard_map/ppermute | solution.py:117
  164.2 9.3 %collective-permute-done.1 = bf16[192,1536]{1,0:T(8,128)(2,1)S(1)} collective-permute-done((bf16[192,1536]{1,0:T(8,128)(2,1)S(1)}, bf16[192,1536]{1,0:T(8,128)(2,1)S(1)}, u32[]{:S(2)}, u32[]{:S(2)}) %collective-permute-start.1) | collective-permute-done | bytes 589856 | tf_op jit(solution)/shard_map/ppermute | solution.py:117
  173.5 9.3 %collective-permute-done.2 = bf16[192,1536]{1,0:T(8,128)(2,1)S(1)} collective-permute-done((bf16[192,1536]{1,0:T(8,128)(2,1)S(1)}, bf16[192,1536]{1,0:T(8,128)(2,1)S(1)}, u32[]{:S(2)}, u32[]{:S(2)}) %collective-permute-start.2) | collective-permute-done | bytes 589856 | tf_op jit(solution)/shard_map/ppermute | solution.py:117
  183.3 2.3 %constant_dynamic-slice_fusion.3 = bf16[192,6144]{1,0:T(8,128)(2,1)} fusion(bf16[192,12288]{1,0:T(8,128)(2,1)S(1)} %constant_dynamic-update-slice_fusion, s32[]{:T(128)S(6)} %select_n.27), kind=kLoop, calls=%fused_computation.64 | loop fusion | bytes 4718596 | tf_op jit(solution)/shard_map/jit(_roll_dynamic)/dynamic_slice | solution.py:118
  (115 shorter events, 12.4 us)
Async XLA Ops:
  7.2 50.5 %all-gather.2.cloned.1.call-start = ((), (), s32[]{:S(2)}) async-start(), calls=%async_computation.1 | async-start | bytes 1769472 | tf_op jit(solution)/shard_map/all_gather | solution.py:97
  8.8 19.0 %copy-start.10 = (s32[192]{0:T(256)S(1)}, s32[192]{0:T(256)}, u32[]{:S(2)}) copy-start(s32[192]{0:T(256)} %param.12) | copy-start | bytes 2308
  8.9 130.6 %reduce-scatter.2.cloned.1.call-start = ((), (), s32[]{:S(2)}) async-start(), calls=%async_computation.2 | async-start | bytes 2949120 | tf_op jit(solution)/shard_map/reduce_scatter | solution.py:108
  66.2 1.7 copy-start.4
  66.2 1.7 copy-start.6
  67.9 1.0 copy-start.5
  67.9 1.0 copy-start.7
  67.9 1.1 copy-start.2
  70.0 0.8 copy-start.3
  77.8 1.7 copy-start.4
  77.8 1.7 copy-start.6
  79.5 1.0 copy-start.5
  79.5 1.0 copy-start.7
  79.5 1.1 copy-start.2
  81.6 0.8 copy-start.3
  89.4 1.7 copy-start.4
  89.4 1.7 copy-start.6
  91.1 1.0 copy-start.5
  91.1 1.0 copy-start.7
  91.1 1.1 copy-start.2
  93.2 0.8 copy-start.3
  108.2 0.7 copy-start.8
  108.2 31.3 %copy-start = (bf16[192,1536]{1,0:T(8,128)(2,1)S(1)}, bf16[192,1536]{1,0:T(8,128)(2,1)}, u32[]{:S(2)}) copy-start(bf16[192,1536]{1,0:T(8,128)(2,1)} %param.13) | copy-start | bytes 1769476
  139.5 14.3 %copy-start.1 = (bf16[192,1536]{1,0:T(8,128)(2,1)S(1)}, bf16[192,1536]{1,0:T(8,128)(2,1)}, u32[]{:S(2)}) copy-start(bf16[192,1536]{1,0:T(8,128)(2,1)} %reduce-scatter.2.cloned.1.call-done) | copy-start | bytes 1769476
  153.8 29.2 %copy-start.9 = (f32[192]{0:T(256)}, f32[192]{0:T(256)S(1)}, u32[]{:S(2)}) copy-start(f32[192]{0:T(256)S(1)} %broadcast_add_fusion) | copy-start | bytes 2308
  154.9 9.3 %collective-permute-start = (bf16[192,1536]{1,0:T(8,128)(2,1)S(1)}, bf16[192,1536]{1,0:T(8,128)(2,1)S(1)}, u32[]{:S(2)}, u32[]{:S(2)}) collective-permute-start(bf16[192,1536]{1,0:T(8,128)(2,1)S(1)} %get-tuple-element.184), channel_id=1, source_target_pairs={{0,1},{1,2},{2,3},{3,0},{4,5},{5,6},{6,7},{7,4},{8,9},{9,10},{10,1... | collective-permute-start | bytes 1769480 | tf_op jit(solution)/shard_map/ppermute | solution.py:117
  164.2 9.3 %collective-permute-start.1 = (bf16[192,1536]{1,0:T(8,128)(2,1)S(1)}, bf16[192,1536]{1,0:T(8,128)(2,1)S(1)}, u32[]{:S(2)}, u32[]{:S(2)}) collective-permute-start(bf16[192,1536]{1,0:T(8,128)(2,1)S(1)} %collective-permute-done), channel_id=1, source_target_pairs={{0,1},{1,2},{2,3},{3,0},{4,5},{5,6},{6,7},{7,4},{8,9},{9,10},{10,1... | collective-permute-start | bytes 1769480 | tf_op jit(solution)/shard_map/ppermute | solution.py:117
  173.5 9.3 %collective-permute-start.2 = (bf16[192,1536]{1,0:T(8,128)(2,1)S(1)}, bf16[192,1536]{1,0:T(8,128)(2,1)S(1)}, u32[]{:S(2)}, u32[]{:S(2)}) collective-permute-start(bf16[192,1536]{1,0:T(8,128)(2,1)S(1)} %collective-permute-done.1), channel_id=1, source_target_pairs={{0,1},{1,2},{2,3},{3,0},{4,5},{5,6},{6,7},{7,4},{8,9},{9,10},{10,1... | collective-permute-start | bytes 1769480 | tf_op jit(solution)/shard_map/ppermute | solution.py:117
Sparse Core Ops, SparseCore 0:
  10.7 46.8 all-gather.1
  108.3 31.1 reduce-scatter.1
